TPU v7x, 32 devices: a 4x4x1 block of a 4x4x8 slice. The times are simulated.
32 devices in a mesh: dp: 1 (over z), cfg: 4 (over y), tp: 8 (over x, core).
Axes of the slice: x: 4, y: 4, z: 1, core: 2. Of those that a mesh axis runs over, the one named last changes fastest.
The devices are a block of a 4x4x8 slice.
Arguments:
- hidden: bfloat16 [4, 4096, 1152], P(('dp', 'cfg'))
- caption: bfloat16 [4, 120, 1152], P(('dp', 'cfg'))
- cap_len: int32 [4], P(('dp', 'cfg'))
- t_block: bfloat16 [2, 6912], P('dp')
- t_embed: bfloat16 [2, 1152], P('dp')
- x_t: float32 [2, 128, 128, 4], P('dp')
- alpha_bar: float32 [2, 2], P('dp')
- mod_table: bfloat16 [2, 6, 1152], replicated
- w_qkv: bfloat16 [2, 1152, 3, 16, 72], P(None, None, None, 'tp')
- w_proj: bfloat16 [2, 16, 72, 1152], P(None, 'tp')
- w_cq: bfloat16 [2, 1152, 16, 72], P(None, None, 'tp')
- w_ckv: bfloat16 [2, 1152, 2, 16, 72], P(None, None, None, 'tp')
- w_cproj: bfloat16 [2, 16, 72, 1152], P(None, 'tp')
- w_fc1: bfloat16 [2, 1152, 4608], P(None, None, 'tp')
- w_fc2: bfloat16 [2, 4608, 1152], P(None, 'tp')
- final_table: bfloat16 [2, 1152], replicated
- w_out: bfloat16 [1152, 32], replicated
- b_out: bfloat16 [32], replicated
Outputs:
- output: float32 [2, 128, 128, 4], P('dp')
All inputs are finite; a program needn't handle non-finite values.
Results may differ from a plain program's by a relative error of at most 0.0132671.
Values are sent between devices in bfloat16 or wider.
A program may use at most 768 MiB of HBM per device.

v0:
```python
import jax
import jax.numpy as jnp
from jax import lax
from jax.sharding import PartitionSpec as P

GUIDANCE = 4.5
LN_EPS = 1e-6


def layer_norm(values):
    mean_val = jnp.mean(values, axis=-1, keepdims=True)
    centered = values - mean_val
    variance = jnp.mean(centered * centered, axis=-1, keepdims=True)
    return centered * lax.rsqrt(variance + LN_EPS)


def attention(queries, key_vecs, values, key_mask):
    qk_scale = queries.shape[-1] ** -0.5
    scores = jnp.einsum('rqhd,rkhd->rhqk', queries, key_vecs, preferred_element_type=jnp.float32) * qk_scale
    if key_mask is not None:
        scores = jnp.where(key_mask, scores, -1e30)
    attn_prob = jax.nn.softmax(scores, axis=-1).astype(jnp.bfloat16)
    return jnp.einsum('rhqk,rkhd->rqhd', attn_prob, values, preferred_element_type=jnp.float32).astype(jnp.bfloat16)


def tp_block(residual, caption, key_mask, mod_rows, w_qkv, w_proj, w_cq, w_ckv, w_cproj, w_fc1, w_fc2):
    attn_in = (layer_norm(residual) * (1.0 + mod_rows[:, None, 1]) + mod_rows[:, None, 0]).astype(jnp.bfloat16)
    qkv_out = jnp.einsum('rnd,dshe->rnshe', attn_in, w_qkv, preferred_element_type=jnp.float32).astype(jnp.bfloat16)
    self_o = attention(qkv_out[:, :, 0], qkv_out[:, :, 1], qkv_out[:, :, 2], None)
    self_part = jnp.einsum('rnhe,hed->rnd', self_o, w_proj, preferred_element_type=jnp.float32).astype(jnp.bfloat16)
    residual = residual + mod_rows[:, None, 2] * lax.psum(self_part, 'tp').astype(jnp.float32)
    cross_q = jnp.einsum('rnd,dhe->rnhe', residual.astype(jnp.bfloat16), w_cq, preferred_element_type=jnp.float32).astype(jnp.bfloat16)
    cross_kv = jnp.einsum('rtd,dshe->rtshe', caption, w_ckv, preferred_element_type=jnp.float32).astype(jnp.bfloat16)
    cross_o = attention(cross_q, cross_kv[:, :, 0], cross_kv[:, :, 1], key_mask)
    cross_part = jnp.einsum('rnhe,hed->rnd', cross_o, w_cproj, preferred_element_type=jnp.float32).astype(jnp.bfloat16)
    residual = residual + lax.psum(cross_part, 'tp').astype(jnp.float32)
    mlp_in = (layer_norm(residual) * (1.0 + mod_rows[:, None, 4]) + mod_rows[:, None, 3]).astype(jnp.bfloat16)
    mlp_hidden = jax.nn.gelu(jnp.einsum('rnd,df->rnf', mlp_in, w_fc1, preferred_element_type=jnp.float32), approximate=True).astype(jnp.bfloat16)
    mlp_part = jnp.einsum('rnf,fd->rnd', mlp_hidden, w_fc2, preferred_element_type=jnp.float32).astype(jnp.bfloat16)
    return residual + mod_rows[:, None, 5] * lax.psum(mlp_part, 'tp').astype(jnp.float32)


def final_layer(residual, final_table, emb_rows, w_out, b_out, side_len):
    shift_scale = final_table.astype(jnp.float32)[None] + emb_rows[:, None]
    final_in = (layer_norm(residual) * (1.0 + shift_scale[:, None, 1]) + shift_scale[:, None, 0]).astype(jnp.bfloat16)
    out_tok = jnp.einsum('rnd,dc->rnc', final_in, w_out, preferred_element_type=jnp.float32) + b_out.astype(jnp.float32)
    n_rows = residual.shape[0]
    grid_side = side_len // 2
    patches = out_tok.reshape(n_rows, grid_side, grid_side, 2, 2, 8)[:, :, :, :, :, :4]
    return patches.transpose(0, 1, 3, 2, 4, 5).reshape(n_rows, side_len, side_len, 4)


def guidance_mix(eps_all):
    n_images = eps_all.shape[0] // 2
    eps_uncond = eps_all[n_images:]
    return eps_uncond + GUIDANCE * (eps_all[:n_images] - eps_uncond)


def ddim_update(guided, x_t, alpha_bar):
    abar_t = alpha_bar[:, 0][:, None, None, None]
    abar_prev = alpha_bar[:, 1][:, None, None, None]
    x_zero = (x_t - jnp.sqrt(1.0 - abar_t) * guided) / jnp.sqrt(abar_t)
    return jnp.sqrt(abar_prev) * x_zero + jnp.sqrt(1.0 - abar_prev) * guided


def solution(mesh):
    row_spec = P(('dp', 'cfg'))
    part_spec = P('dp')
    in_specs = (row_spec, row_spec, row_spec, part_spec, part_spec, part_spec, part_spec, P(),
                P(None, None, None, 'tp'), P(None, 'tp'), P(None, None, 'tp'), P(None, None, None, 'tp'),
                P(None, 'tp'), P(None, None, 'tp'), P(None, 'tp'), P(), P(), P())

    def local_step(hidden, caption, cap_len, t_block, t_embed, x_t, alpha_bar, mod_table, w_qkv, w_proj, w_cq, w_ckv, w_cproj, w_fc1, w_fc2, final_table, w_out, b_out):
        n_rows = hidden.shape[0]
        model_dim = hidden.shape[2]
        row_start = (lax.axis_index('cfg') * n_rows) % t_block.shape[0]
        t_rows = lax.dynamic_slice_in_dim(t_block, row_start, n_rows, axis=0).astype(jnp.float32).reshape(n_rows, 6, model_dim)
        emb_rows = lax.dynamic_slice_in_dim(t_embed, row_start, n_rows, axis=0).astype(jnp.float32)
        key_mask = (jnp.arange(caption.shape[1])[None, :] < cap_len[:, None])[:, None, None, :]
        residual = hidden.astype(jnp.float32)
        for layer_idx in range(mod_table.shape[0]):
            mod_rows = mod_table[layer_idx].astype(jnp.float32)[None] + t_rows
            residual = tp_block(residual, caption, key_mask, mod_rows, w_qkv[layer_idx], w_proj[layer_idx], w_cq[layer_idx], w_ckv[layer_idx], w_cproj[layer_idx], w_fc1[layer_idx], w_fc2[layer_idx])
        eps_local = final_layer(residual, final_table, emb_rows, w_out, b_out, x_t.shape[1])
        eps_all = lax.all_gather(eps_local, 'cfg', axis=0, tiled=True)
        return ddim_update(guidance_mix(eps_all), x_t, alpha_bar)

    return jax.shard_map(local_step, mesh=mesh, in_specs=in_specs, out_specs=part_spec, check_vma=False)
```

profile of v0, /device:TPU:97, one launch (start us, length us, event | category | flops | bytes accessed | tf_op | source)
XLA Modules:
  0.0 1157.4 jit_solution(4144219533679447876)
XLA Ops:
  6.6 5.1 convert_reduce_fusion
  11.7 1.2 copy-done.1
  13.0 2.6 fusion.16
  15.8 1.1 fusion.186
  16.9 0.7 slice_reduce_fusion.2
  17.7 8.3 fusion.65
  26.0 2.3 convert_bitcast_fusion.1
  28.2 56.5 %fusion.190 = (f32[2,4096]{1,0:T(2,128)S(1)}, f32[2,4096,4096]{1,2,0:T(8,128)}) fusion(bf16[1,4096,3,2,72]{1,4,3,2,0:T(8,128)(2,1)} %convert_bitcast_fusion.1), kind=kOutput, calls=%fused_computation.239 | convolution fusion | flops 4932505600 | bytes 136609792 | tf_op jit(solution)/shard_map/sub | solution.py:22
  84.7 42.6 %fusion.116 = bf16[4096,2,72]{0,2,1:T(8,128)(2,1)S(1)} fusion(f32[2,4096,4096]{1,2,0:T(8,128)} %get-tuple-element.38, f32[2,4096]{1,0:T(2,128)S(1)} %get-tuple-element.37, bf16[1,4096,3,2,72]{1,4,3,2,0:T(8,128)(2,1)} %convert_bitcast_fusion.1), kind=kOutput, calls=%fused_computation.127 | convolution fusion | flops 4899536896 | bytes 136609792 | tf_op jit(solution)/shard_map/rhqk,rkhd->rqhd/dot_general | solution.py:23
  127.4 5.4 fusion.27
  132.8 0.5 all-reduce.9.cloned.1.call-start
  134.0 0.9 fusion.187
  135.4 0.8 fusion.188
  136.2 109.3 %all-reduce.7.cloned.1.call-done = bf16[1,4096,1152]{2,1,0:T(8,128)(2,1)} async-done(((bf16[1,4096,1152]{2,1,0:T(8,128)(2,1)}), bf16[1,4096,1152]{2,1,0:T(8,128)(2,1)}) %all-reduce.7.cloned.1.call-update) | async-done | bytes 9437200 | tf_op jit(solution)/shard_map/psum | solution.py:31
  245.4 11.4 fusion.52
  256.8 5.2 fusion.191
  262.0 9.0 fusion.28
  271.1 108.7 %all-reduce.9.cloned.1.call-done = bf16[1,4096,1152]{2,1,0:T(8,128)(2,1)} async-done(((bf16[1,4096,1152]{2,1,0:T(8,128)(2,1)}), bf16[1,4096,1152]{2,1,0:T(8,128)(2,1)}) %all-reduce.9.cloned.1.call-update) | async-done | bytes 9437200 | tf_op jit(solution)/shard_map/psum | solution.py:36
  379.8 10.9 fusion.183
  390.8 0.9 copy-done.2
  391.7 9.4 multiply_reduce_fusion.5
  401.1 23.8 %fusion.25 = bf16[1,4096,1152]{2,1,0:T(8,128)(2,1)} fusion(f32[1152]{0:T(1024)S(1)} %copy-done.22, f32[1152]{0:T(1024)S(1)} %copy-done.21, f32[4096]{0:T(1024)S(1)} %add_rsqrt_fusion.3, f32[4096]{0:T(1024)S(1)} %broadcast_multiply_fusion.3, bf16[2,576,1152]{2,1,0:T(8,128)(2,1)} %param.32, bf16[2,1152,576]{1,2,0:T(8,128)(2,1)} %param.31, ...), kind=kOutput, calls=%fused_computation.49 | convolution fusion | flops 10949492736 | bytes 40449536 | tf_op jit(solution)/shard_map/rnf,fd->rnd/dot_general | solution.py:39
  425.2 108.5 %all-reduce.11.cloned.1.call-done = bf16[1,4096,1152]{2,1,0:T(8,128)(2,1)} async-done(((bf16[1,4096,1152]{2,1,0:T(8,128)(2,1)}), bf16[1,4096,1152]{2,1,0:T(8,128)(2,1)}) %all-reduce.11.cloned.1.call-update) | async-done | bytes 9437200 | tf_op jit(solution)/shard_map/psum | solution.py:40
  533.7 20.2 %fusion.185 = (f32[4096]{0:T(1024)S(1)}, f32[1,4096,1152]{2,1,0:T(8,128)}) fusion(bf16[1,4096,1152]{2,1,0:T(8,128)(2,1)} %all-reduce.11.cloned.1.call-done, f32[1152]{0:T(1024)S(1)} %copy-done.15, bf16[1,4096,1152]{2,1,0:T(8,128)(2,1)} %all-reduce.9.cloned.1.call-done, bf16[1,4096,1152]{2,1,0:T(8,128)(2,1)} %all-reduce.7.cloned.1.call-done, ...), kind=kLoop, calls=%fused_computation.234 | loop fusion | flops 47181824 | bytes 56648704 | tf_op jit(solution)/shard_map/reduce_sum | solution.py:11
  553.9 8.5 multiply_reduce_fusion.4
  562.4 10.1 fusion.58
  572.5 2.3 convert_bitcast_fusion
  574.9 56.5 %fusion.194 = (f32[2,4096]{1,0:T(2,128)S(1)}, f32[2,4096,4096]{1,2,0:T(8,128)}) fusion(bf16[1,4096,3,2,72]{1,4,3,2,0:T(8,128)(2,1)} %convert_bitcast_fusion), kind=kOutput, calls=%fused_computation.241 | convolution fusion | flops 4932505600 | bytes 136609792 | tf_op jit(solution)/shard_map/sub | solution.py:22
  631.4 43.5 %fusion.117 = bf16[4096,2,72]{0,2,1:T(8,128)(2,1)} fusion(f32[2,4096,4096]{1,2,0:T(8,128)} %get-tuple-element.42, f32[2,4096]{1,0:T(2,128)S(1)} %get-tuple-element.41, bf16[1,4096,3,2,72]{1,4,3,2,0:T(8,128)(2,1)} %convert_bitcast_fusion), kind=kOutput, calls=%fused_computation.128 | convolution fusion | flops 4899536896 | bytes 136609792 | tf_op jit(solution)/shard_map/rhqk,rkhd->rqhd/dot_general | solution.py:23
  674.9 8.0 fusion.29
  683.4 108.3 %all-reduce.13.cloned.1.call-done = bf16[1,4096,1152]{2,1,0:T(8,128)(2,1)} async-done(((bf16[1,4096,1152]{2,1,0:T(8,128)(2,1)}), bf16[1,4096,1152]{2,1,0:T(8,128)(2,1)}) %all-reduce.13.cloned.1.call-update) | async-done | bytes 9437200 | tf_op jit(solution)/shard_map/psum | solution.py:31
  791.7 10.8 fusion.33
  802.5 3.6 fusion.195
  806.1 9.2 fusion.30
  815.4 108.7 %all-reduce.15.cloned.1.call-done = bf16[1,4096,1152]{2,1,0:T(8,128)(2,1)} async-done(((bf16[1,4096,1152]{2,1,0:T(8,128)(2,1)}), bf16[1,4096,1152]{2,1,0:T(8,128)(2,1)}) %all-reduce.15.cloned.1.call-update) | async-done | bytes 9437200 | tf_op jit(solution)/shard_map/psum | solution.py:36
  924.1 20.1 %fusion.184 = (f32[4096]{0:T(1024)S(1)}, f32[1,4096,1152]{2,1,0:T(8,128)}) fusion(bf16[1,4096,1152]{2,1,0:T(8,128)(2,1)} %all-reduce.15.cloned.1.call-done, f32[1,4096,1152]{2,1,0:T(8,128)} %get-tuple-element.26, bf16[1,4096,1152]{2,1,0:T(8,128)(2,1)} %all-reduce.13.cloned.1.call-done, f32[1152]{0:T(1024)S(1)} %copy-done.11), kind=kLoop, calls=%fused_computation.233 | loop fusion | flops 28307456 | bytes 56644096 | tf_op jit(solution)/shard_map/reduce_sum | solution.py:11
  944.2 8.5 multiply_reduce_fusion.3
  952.8 20.3 %fusion.26 = bf16[1,4096,1152]{2,1,0:T(8,128)(2,1)} fusion(f32[1,4096,1152]{2,1,0:T(8,128)} %get-tuple-element.24, f32[1152]{0:T(1024)S(1)} %copy-done.17, f32[1152]{0:T(1024)S(1)} %copy-done.18, f32[4096]{0:T(1024)S(1)} %add_rsqrt_fusion.1, f32[4096]{0:T(1024)S(1)} %broadcast_multiply_fusion.1, bf16[2,576,1152]{2,1,0:T(8,128)(2,1)S(1)} %copy-done.26, ...), kind=kOutput, calls=%fused_computation.50 | convolution fusion | flops 10921181184 | bytes 31014912 | tf_op jit(solution)/shard_map/rnf,fd->rnd/dot_general | solution.py:39
  973.3 0.5 copy-done.31
  973.9 108.1 %all-reduce.17.cloned.1.call-done = bf16[1,4096,1152]{2,1,0:T(8,128)(2,1)} async-done(((bf16[1,4096,1152]{2,1,0:T(8,128)(2,1)}), bf16[1,4096,1152]{2,1,0:T(8,128)(2,1)}) %all-reduce.17.cloned.1.call-update) | async-done | bytes 9437200 | tf_op jit(solution)/shard_map/psum | solution.py:40
  1082.0 12.4 %fusion.93 = f32[4096]{0:T(1024)S(1)} fusion(f32[1,4096,1152]{2,1,0:T(8,128)} %get-tuple-element.24, bf16[1,4096,1152]{2,1,0:T(8,128)(2,1)} %all-reduce.17.cloned.1.call-done, f32[1152]{0:T(1024)S(1)} %copy-done.14), kind=kLoop, calls=%fused_computation.112 | loop fusion | flops 18870272 | bytes 28332544 | tf_op jit(solution)/shard_map/reduce_sum | solution.py:11
  1094.5 10.2 multiply_reduce_fusion.2
  1105.0 7.8 fusion.118
  1113.3 8.8 copy.47
  1122.1 5.9 copy.40
  1128.3 19.2 %all-gather.2.cloned.1.call-done = f32[4,128,128,4]{2,1,3,0:T(8,128)} async-done(((f32[1,128,128,4]{2,1,3,0:T(8,128)}), f32[4,128,128,4]{2,1,3,0:T(8,128)}) %all-gather.2.cloned.1.call-update) | async-done | bytes 1048592 | tf_op jit(solution)/shard_map/all_gather | solution.py:85
  1147.5 1.4 fusion.141
  1148.9 1.1 copy.42
  (115 shorter events, 3.0 us)
Async XLA Ops:
  6.5 128.4 %copy-start = (bf16[1,120,1152]{2,1,0:T(8,128)(2,1)S(1)}, bf16[1,120,1152]{2,1,0:T(8,128)(2,1)}, u32[]{:S(2)}) copy-start(bf16[1,120,1152]{2,1,0:T(8,128)(2,1)} %param.19) | copy-start | bytes 829444
  6.6 238.9 %all-reduce.7.cloned.1.call-start = ((), (), s32[]{:S(2)}) async-start(), calls=%async_computation | async-start | bytes 18874368 | tf_op jit(solution)/shard_map/psum | solution.py:31
  6.6 6.4 copy-start.1
  6.6 9.0 copy-start.16
  6.6 9.2 copy-start.13
  6.6 9.2 copy-start.5
  84.7 42.7 %copy-start.27 = (bf16[2,2,72,1152]{3,2,1,0:T(8,128)(2,1)S(1)}, bf16[2,2,72,1152]{3,2,1,0:T(8,128)(2,1)}, u32[]{:S(2)}) copy-start(bf16[2,2,72,1152]{3,2,1,0:T(8,128)(2,1)} %param.27) | copy-start | bytes 1990660
  127.4 6.6 copy-start.7
  132.8 2.6 copy-start.9
  132.8 112.6 %copy-start.12 = (f32[1152]{0:T(1024)S(1)}, f32[1152]{0:T(1024)}, u32[]{:S(2)}) copy-start(f32[1152]{0:T(1024)} %get-tuple-element.45) | copy-start | bytes 13828
  132.8 247.0 %all-reduce.9.cloned.1.call-start = ((), (), s32[]{:S(2)}) async-start(), calls=%async_computation.1 | async-start | bytes 18874368 | tf_op jit(solution)/shard_map/psum | solution.py:36
  134.0 122.7 %copy-start.32 = (pred[120]{0:T(512)(128)(4,1)}, pred[120]{0:T(512)(128)(4,1)S(1)}, u32[]{:S(2)}) copy-start(pred[120]{0:T(512)(128)(4,1)S(1)} %iota_compare_fusion) | copy-start | bytes 364
  245.4 16.6 %copy-start.29 = (bf16[2,2,72,1152]{3,2,1,0:T(8,128)(2,1)S(1)}, bf16[2,2,72,1152]{3,2,1,0:T(8,128)(2,1)}, u32[]{:S(2)}) copy-start(bf16[2,2,72,1152]{3,2,1,0:T(8,128)(2,1)} %param.30) | copy-start | bytes 1990660
  271.1 262.6 %all-reduce.11.cloned.1.call-start = ((), (), s32[]{:S(2)}) async-start(), calls=%async_computation.2 | async-start | bytes 18874368 | tf_op jit(solution)/shard_map/psum | solution.py:40
  379.8 11.8 %copy-start.2 = (bf16[1,4096,1152]{2,1,0:T(8,128)(2,1)S(1)}, bf16[1,4096,1152]{2,1,0:T(8,128)(2,1)}, u32[]{:S(2)}) copy-start(bf16[1,4096,1152]{2,1,0:T(8,128)(2,1)} %all-reduce.9.cloned.1.call-done) | copy-start | bytes 28311556
  391.7 9.4 copy-start.21
  391.7 9.4 copy-start.22
  424.8 108.8 %copy-start.15 = (f32[1152]{0:T(1024)S(1)}, f32[1152]{0:T(1024)}, u32[]{:S(2)}) copy-start(f32[1152]{0:T(1024)} %get-tuple-element.50) | copy-start | bytes 13828
  424.9 366.8 %all-reduce.13.cloned.1.call-start = ((), (), s32[]{:S(2)}) async-start(), calls=%async_computation.3 | async-start | bytes 18874368 | tf_op jit(solution)/shard_map/psum | solution.py:31
  553.9 8.5 copy-start.8
  553.9 8.5 copy-start.19
  553.9 8.5 copy-start.20
  631.4 43.5 %copy-start.28 = (bf16[2,2,72,1152]{3,2,1,0:T(8,128)(2,1)S(1)}, bf16[2,2,72,1152]{3,2,1,0:T(8,128)(2,1)}, u32[]{:S(2)}) copy-start(bf16[2,2,72,1152]{3,2,1,0:T(8,128)(2,1)} %param.27) | copy-start | bytes 1990660
  674.9 8.1 copy-start.4
  674.9 116.8 %copy-start.6 = (bf16[1,1152,2,72]{1,3,2,0:T(8,128)(2,1)S(1)}, bf16[1,1152,2,72]{1,3,2,0:T(8,128)(2,1)}, u32[]{:S(2)}) copy-start(bf16[1,1152,2,72]{1,3,2,0:T(8,128)(2,1)} %get-tuple-element.32) | copy-start | bytes 995332
  674.9 116.8 %copy-start.11 = (f32[1152]{0:T(1024)S(1)}, f32[1152]{0:T(1024)}, u32[]{:S(2)}) copy-start(f32[1152]{0:T(1024)} %get-tuple-element.10) | copy-start | bytes 13828
  682.9 241.2 %all-reduce.15.cloned.1.call-start = ((), (), s32[]{:S(2)}) async-start(), calls=%async_computation.4 | async-start | bytes 18874368 | tf_op jit(solution)/shard_map/psum | solution.py:36
  791.7 10.8 copy-start.33
  815.4 266.6 %all-reduce.17.cloned.1.call-start = ((), (), s32[]{:S(2)}) async-start(), calls=%async_computation.5 | async-start | bytes 18874368 | tf_op jit(solution)/shard_map/psum | solution.py:40
  944.2 8.6 copy-start.17
  944.2 8.6 copy-start.18
  944.2 8.6 copy-start.26
  973.2 0.7 copy-start.31
  973.2 0.7 copy-start.23
  973.2 0.7 copy-start.24
  973.2 108.9 %copy-start.14 = (f32[1152]{0:T(1024)S(1)}, f32[1152]{0:T(1024)}, u32[]{:S(2)}) copy-start(f32[1152]{0:T(1024)} %get-tuple-element.5) | copy-start | bytes 13828
  973.2 174.3 %all-gather.2.cloned.1.call-start = ((), (), s32[]{:S(2)}) async-start(), calls=%async_computation.6 | async-start | bytes 1310720 | tf_op jit(solution)/shard_map/all_gather | solution.py:85
  1082.0 12.4 %copy-start.3 = (bf16[1,4096,1152]{2,1,0:T(8,128)(2,1)S(1)}, bf16[1,4096,1152]{2,1,0:T(8,128)(2,1)}, u32[]{:S(2)}) copy-start(bf16[1,4096,1152]{2,1,0:T(8,128)(2,1)} %all-reduce.17.cloned.1.call-done) | copy-start | bytes 28311556
  1082.0 22.7 %slice-start = ((s8[18874368]{0:T(1024)(128)(4,1)}), s8[4194304]{0:T(1024)(128)(4,1)S(1)}, s32[]{:S(2)}) async-start(s8[18874368]{0:T(1024)(128)(4,1)} %bitcast.247), calls=%async_computation.7 | async-start | bytes 8388608
  1082.0 22.7 %slice-start.1 = ((s8[18874368]{0:T(1024)(128)(4,1)}), s8[4194304]{0:T(1024)(128)(4,1)S(1)}, s32[]{:S(2)}) async-start(s8[18874368]{0:T(1024)(128)(4,1)} %bitcast.247), calls=%async_computation.8 | async-start | bytes 8388608
  1082.0 22.7 %slice-start.2 = ((s8[18874368]{0:T(1024)(128)(4,1)}), s8[4194304]{0:T(1024)(128)(4,1)S(1)}, s32[]{:S(2)}) async-start(s8[18874368]{0:T(1024)(128)(4,1)} %bitcast.247), calls=%async_computation.9 | async-start | bytes 8388608
  1094.4 10.3 slice-start.3
  1094.4 10.5 slice-start.4
  1094.5 10.5 copy-start.30
  1113.2 14.8 %copy-start.25 = (f32[2,2]{1,0:T(2,128)S(1)}, f32[2,2]{1,0:T(2,128)}, u32[]{:S(2)}) copy-start(f32[2,2]{1,0:T(2,128)} %param.24) | copy-start | bytes 52
  1113.3 34.3 %copy-start.10 = (f32[2,128,128,4]{2,3,1,0:T(4,128)S(1)}, f32[2,128,128,4]{2,3,1,0:T(4,128)}, u32[]{:S(2)}) copy-start(f32[2,128,128,4]{2,3,1,0:T(4,128)} %param.23) | copy-start | bytes 1572868
Sparse Core Ops, SparseCore 0:
  132.9 112.4 all-reduce.6
  271.2 108.6 all-reduce.8
  425.0 108.6 all-reduce.10
  683.0 108.6 all-reduce.12
  815.5 108.6 all-reduce.14
  973.4 108.6 all-reduce.16
  1128.1 19.3 all-gather.1
where the time goes:
time: 1160 us
  waiting for transfers between devices  671 us (58%)
  matrix products  333 us (29%)
  other arithmetic  115 us (10%)
  local copies, waits for them, and re-layouts  22.2 us (2%)
  between operations  15.3 us (1%)
    psum x2, waiting for transfers between devices, tp_block(): lax.psum(self_part, 'tp').astype(jnp.float32)  218 us
    psum x2, waiting for transfers between devices, tp_block(): residual = residual + lax.psum(cross_part, 'tp').astype(jnp.float32)  217 us
    psum x2, waiting for transfers between devices, tp_block(): lax.psum(mlp_part, 'tp').astype(jnp.float32)  217 us
    sub x4, matrix products, attention(): attn_prob = jax.nn.softmax(scores, axis=-1).astype(jnp.bfloat16)  122 us
    dot_general x2, matrix products, attention(): jnp.einsum('rhqk,rkhd->rqhd', attn_prob, values, preferred_element_type=j...  86.1 us
    reduce_sum x5, other arithmetic, layer_norm(): mean_val = jnp.mean(values, axis=-1, keepdims=True)  68.7 us
    dot_general x2, matrix products, tp_block(): jnp.einsum('rnf,fd->rnd', mlp_hidden, w_fc2, preferred_element_type=jnp.f...  44.1 us
    unnamed x6, matrix products  41.2 us
  transfers between devices with their start and end apart: 7, of which 7 were waited for; matrix products, arithmetic and copies ran while one was open for 0% of the time, Pallas kernels for 0%

commit v1 on v0

v1 whole, which is shorter than its diff:
```python
import functools

import jax
import jax.numpy as jnp
from jax import lax
from jax.experimental import pallas as pl
from jax.experimental.pallas import tpu as pltpu
from jax.sharding import PartitionSpec as P

GUIDANCE = 4.5
LN_EPS = 1e-6
LOG2E = 1.4426950408889634
MESH = pl.DeviceIdType.MESH
BF16 = jnp.bfloat16
F32 = jnp.float32
K_ROWS = 512
F_ROWS = 768


def layer_norm(values):
    mean_val = jnp.mean(values, axis=-1, keepdims=True)
    centered = values - mean_val
    variance = jnp.mean(centered * centered, axis=-1, keepdims=True)
    return centered * lax.rsqrt(variance + LN_EPS)


def dot32(spec, left, right):
    return jnp.einsum(spec, left, right, preferred_element_type=F32)


ROW_W = ('kv', 'proj', 'cq', 'cproj')
GRID_W = ('fc1', 'fc2')
EAST = {'kv': False, 'proj': True, 'cq': True, 'cproj': False, 'fc1': True, 'fc2': False}


class Wires:
    def __init__(self, send_sem, recv_sem):
        self.send_sem, self.recv_sem, self.ids, self.sent = send_sem, recv_sem, {}, []

    def idx(self, key):
        return self.ids.setdefault(key, len(self.ids))

    def copy(self, key, src, dst, dev):
        k = self.idx(key)
        return pltpu.make_async_remote_copy(src_ref=src, dst_ref=dst, send_sem=self.send_sem.at[k],
                                            recv_sem=self.recv_sem.at[k], device_id=dev, device_id_type=MESH)

    def start(self, key, src, dst, dev):
        self.sent.append((key, src, dst, dev))
        self.copy(key, src, dst, dev).start()

    def arrived(self, key, region, dev):
        self.copy(key, region, region, dev).wait_recv()

    def drain(self):
        for item in self.sent:
            self.copy(*item).wait_send()


def attn_kernel(n_tp, n_cfg, head_dim, scale, norm, a_in, w_ref, mod_ref, kv_in, proj_in, cq_in, cproj_in, fc1_in, fc2_in,
                out_o, kv_g, proj_g, cq_g, cproj_g, fc1_g, fc2_g,
                o_buf, a_buf, q_ref, k_ref, v_ref, send_sem, recv_sem, o_send, o_recv, loc_sem, a_sem):
    me = lax.axis_index('tp')
    row = lax.axis_index('cfg')
    east, west, opp = lax.rem(me + 2, n_tp), lax.rem(me + n_tp - 2, n_tp), lax.rem(me + 4, n_tp)
    mate = me + 1 - 2 * lax.rem(me, 2)
    flip = lambda idx: idx + 1 - 2 * lax.rem(idx, 2)
    north, south, far = lax.rem(row + 1, n_cfg), lax.rem(row + n_cfg - 1, n_cfg), lax.rem(row + 2, n_cfg)
    to_east, to_west, to_mate = {'tp': east}, {'tp': west}, {'tp': mate}
    to_north, to_south = {'cfg': north}, {'cfg': south}
    src = dict(kv=kv_in, proj=proj_in, cq=cq_in, cproj=cproj_in, fc1=fc1_in, fc2=fc2_in)
    full = dict(kv=kv_g, proj=proj_g, cq=cq_g, cproj=cproj_g, fc1=fc1_g, fc2=fc2_g)
    wires = Wires(send_sem, recv_sem)
    n_chunk, _, chunk_rows = o_buf.shape
    n_heads = v_ref.shape[0]
    width = n_heads * head_dim

    barrier = pltpu.get_barrier_semaphore()
    for step in range(1, n_tp):
        pl.semaphore_signal(barrier, inc=1, device_id={'tp': lax.rem(me + step, n_tp)}, device_id_type=MESH)
    for dev in (to_north, to_south):
        pl.semaphore_signal(barrier, inc=1, device_id=dev, device_id_type=MESH)
    pl.semaphore_wait(barrier, n_tp + 1)

    def o_copy(step):
        there = lax.rem(me + 1 + step, n_tp)
        return pltpu.make_async_remote_copy(src_ref=o_buf.at[step], dst_ref=out_o.at[me], send_sem=o_send.at[step],
                                            recv_sem=o_recv.at[step], device_id={'tp': there}, device_id_type=MESH)

    o_local = pltpu.make_async_copy(o_buf.at[n_tp - 1], out_o.at[me], loc_sem)

    def spread_y(name, shard, tag):
        part = full[name].at[shard, row]
        wires.start(('y', name, tag, 'N'), part, part, to_north)
        wires.start(('y', name, tag, 'S'), part, part, to_south)

    def hand_mate(key, part):
        wires.start(('d',) + key, part, part, to_mate)

    def ev_first():
        for name in GRID_W:
            wires.start(('x', name, 'E'), src[name].at[row], full[name].at[me, row], to_east)
            wires.start(('x', name, 'W'), src[name].at[row], full[name].at[me, row], to_west)
        for name in GRID_W + ROW_W:
            wires.start(('own', name), src[name], full[name].at[me], to_mate)

    def ev_x_near(name):
        wires.arrived(('x', name, 'E'), full[name].at[west, row], to_west)
        wires.arrived(('x', name, 'W'), full[name].at[east, row], to_east)
        part = full[name].at[west if EAST[name] else east, row]
        wires.start(('xf', name), part, part, to_east if EAST[name] else to_west)
        for shard, tag in ((west, 'w'), (east, 'e')):
            spread_y(name, shard, tag)
            hand_mate((name, tag, 0), full[name].at[shard, row])

    def ev_row_first():
        for name in ROW_W:
            wires.start(('x', name, 'E'), src[name], full[name].at[me], to_east)
            wires.start(('x', name, 'W'), src[name], full[name].at[me], to_west)

    def ev_x_opp():
        for name in GRID_W:
            wires.arrived(('xf', name), full[name].at[opp, row], to_west if EAST[name] else to_east)
            spread_y(name, opp, 'o')
            hand_mate((name, 'o', 0), full[name].at[opp, row])

    def ev_y(shard, tag):
        for name in GRID_W:
            wires.arrived(('y', name, tag, 'N'), full[name].at[shard, south], to_south)
            wires.arrived(('y', name, tag, 'S'), full[name].at[shard, north], to_north)
            part = full[name].at[shard, south if EAST[name] else north]
            wires.start(('yf', name, tag), part, part, to_north if EAST[name] else to_south)
            hand_mate((name, tag, 1), full[name].at[shard, south])
            hand_mate((name, tag, 2), full[name].at[shard, north])

    def ev_row_near():
        for name in ROW_W:
            wires.arrived(('x', name, 'E'), full[name].at[west], to_west)
            wires.arrived(('x', name, 'W'), full[name].at[east], to_east)
            part = full[name].at[west if EAST[name] else east]
            wires.start(('xf', name), part, part, to_east if EAST[name] else to_west)
            hand_mate((name, 'w', 0), full[name].at[west])
            hand_mate((name, 'e', 0), full[name].at[east])
        for name in GRID_W + ROW_W:
            wires.arrived(('own', name), full[name].at[mate], to_mate)
            wires.start(('back', name), full[name].at[mate], full[name].at[mate], to_mate)

    def ev_row_opp():
        for name in ROW_W:
            wires.arrived(('xf', name), full[name].at[opp], to_west if EAST[name] else to_east)
            hand_mate((name, 'o', 0), full[name].at[opp])

    def ev_y_far(shard, tag):
        for name in GRID_W:
            wires.arrived(('yf', name, tag), full[name].at[shard, far], to_south if EAST[name] else to_north)
            hand_mate((name, tag, 3), full[name].at[shard, far])

    def ev_second():
        ev_x_near('fc2')
        ev_row_first()

    ev_first()
    loads = [pltpu.make_async_copy(a_in.at[pl.ds(i * chunk_rows, chunk_rows)], a_buf.at[i], a_sem.at[i]) for i in range(n_chunk)]
    for load in loads:
        load.start()
    for load in loads:
        load.wait()
    v_ref[:, head_dim:] = jnp.ones((n_heads, v_ref.shape[1] - head_dim, v_ref.shape[2]), BF16)

    def project(at, carry):
        act = a_buf[at]
        if norm:
            act = (layer_norm(act.astype(F32)) * (1.0 + mod_ref[1:2]) + mod_ref[0:1]).astype(BF16)
        cols = pl.ds(pl.multiple_of(at * chunk_rows, chunk_rows), chunk_rows)
        across = (((1,), (1,)), ((), ()))
        q_ref[:, cols] = lax.dot_general(w_ref[0], act, across, preferred_element_type=F32).astype(BF16)
        k_ref[cols] = lax.dot_general(act, w_ref[1], across, preferred_element_type=F32).astype(BF16)
        vals = lax.dot_general(w_ref[2], act, across, preferred_element_type=F32).astype(BF16)
        for h in range(n_heads):
            v_ref[h, :head_dim, cols] = vals[h * head_dim:(h + 1) * head_dim]
        if norm:
            pl.when(at == 5)(lambda: ev_x_near('fc1'))
        return carry

    lax.fori_loop(0, n_chunk, project, 0)
    if norm:
        ev_second()
        events = {0: ev_x_opp, 2: lambda: ev_y(west, 'w'), 3: lambda: ev_y(east, 'e'), 5: ev_row_near}
    else:
        ev_x_near('fc1')
        events = {0: ev_second, 1: ev_x_opp, 3: lambda: ev_y(west, 'w'), 4: lambda: ev_y(east, 'e'), 6: ev_row_near}
    row_ids = lax.broadcasted_iota(jnp.int32, (width, chunk_rows), 0)

    def attend(step, carry):
        chunk = lax.rem(me + 1 + step, n_tp)
        q_all = q_ref[:, pl.ds(pl.multiple_of(chunk * chunk_rows, chunk_rows), chunk_rows)]
        queries = [jnp.where((row_ids >= h * head_dim) & (row_ids < (h + 1) * head_dim), q_all, 0) for h in range(n_heads)]
        units = [(h, j) for j in range(k_ref.shape[0] // K_ROWS) for h in range(n_heads)]
        score = lambda unit: jnp.dot(k_ref[pl.ds(unit[1] * K_ROWS, K_ROWS)], queries[unit[0]], preferred_element_type=F32)
        top, mixed = [None] * n_heads, [None] * n_heads
        scores = score(units[0])
        for at, (h, j) in enumerate(units):
            ahead = score(units[at + 1]) if at + 1 < len(units) else None
            peak = jnp.max(scores, axis=0, keepdims=True)
            if j:
                peak = jnp.maximum(peak, top[h])
                fade = jnp.exp2((top[h] - peak) * (scale * LOG2E))
            top[h] = peak
            probs = jnp.exp2((scores - peak) * (scale * LOG2E)).astype(BF16)
            term = jnp.dot(v_ref[h, :, pl.ds(j * K_ROWS, K_ROWS)], probs, preferred_element_type=F32)
            mixed[h] = mixed[h] * fade + term if j else term
            scores = ahead
        outs = [part[:head_dim] / part[head_dim:head_dim + 1] for part in mixed]
        o_buf[step] = jnp.concatenate(outs, axis=0).astype(BF16)

        @pl.when(step < n_tp - 1)
        def _():
            o_copy(step).start()
        for when, event in events.items():
            pl.when(step == when)(event)
        return carry

    lax.fori_loop(0, n_chunk, attend, 0)
    o_local.start()
    ev_y(opp, 'o')
    ev_row_opp()
    for shard, tag in ((west, 'w'), (east, 'e'), (opp, 'o')):
        ev_y_far(shard, tag)
    for name in GRID_W:
        for shard, tag in ((west, 'w'), (east, 'e'), (opp, 'o')):
            for part, at_row in enumerate((row, south, north, far)):
                wires.arrived(('d', name, tag, part), full[name].at[flip(shard), at_row], to_mate)
    for name in ROW_W:
        for shard, tag in ((west, 'w'), (east, 'e'), (opp, 'o')):
            wires.arrived(('d', name, tag, 0), full[name].at[flip(shard)], to_mate)
    for name in GRID_W + ROW_W:
        wires.arrived(('back', name), full[name].at[me], to_mate)
    wires.drain()
    for step in range(n_tp - 1):
        origin = lax.rem(me + n_tp - 1 - step, n_tp)
        o_copy(step).wait_send()
        pltpu.make_async_remote_copy(src_ref=out_o.at[origin], dst_ref=out_o.at[origin], send_sem=o_send.at[step],
                                     recv_sem=o_recv.at[step], device_id={'tp': origin}, device_id_type=MESH).wait_recv()
    o_local.wait()


N_WIRES = 6 + 12 + 6 + 12 + 6 + 24 + 12 + 6


def attend_and_gather(mesh, layer, norm, n_heads, act, w_t, mods, kv, shards):
    n_tp, n_cfg = mesh.shape['tp'], mesh.shape['cfg']
    n_tok, dim = act.shape
    width = w_t.shape[1]
    head_dim = width // n_heads
    vmem = pl.BlockSpec(memory_space=pltpu.VMEM)
    hbm = pl.BlockSpec(memory_space=pl.ANY)
    sem = pltpu.SemaphoreType.DMA
    out_shape = [jax.ShapeDtypeStruct((n_tp, width, n_tok // n_tp), BF16)]
    out_shape += [jax.ShapeDtypeStruct((n_tp,) + shard.shape, BF16) for shard in (kv,) + shards]
    return pl.pallas_call(
        functools.partial(attn_kernel, n_tp, n_cfg, head_dim, head_dim ** -0.5, norm),
        out_shape=out_shape,
        in_specs=[hbm, vmem, vmem] + [hbm] * 6,
        out_specs=[hbm] * 7,
        scratch_shapes=[pltpu.VMEM((n_tp, width, n_tok // n_tp), BF16), pltpu.VMEM((n_tp, n_tok // n_tp, dim), BF16),
                        pltpu.VMEM((width, n_tok), BF16), pltpu.VMEM((n_tok, width), BF16), pltpu.VMEM((n_heads, head_dim + 8, n_tok), BF16),
                        sem((N_WIRES,)), sem((N_WIRES,)), sem((n_tp - 1,)), sem((n_tp - 1,)), sem, sem((n_tp,))],
        compiler_params=pltpu.CompilerParams(collective_id=layer, has_side_effects=True, vmem_limit_bytes=60 << 20),
        name=f'attend_gather_{layer}',
    )(act, w_t, mods, kv, *shards)


def mlp_kernel(res_ref, mod_ref, w1_ref, w2_ref, out_ref, next_ref, a_buf, total):
    at = pl.program_id(0)

    @pl.when(at == 0)
    def _():
        a_buf[...] = (layer_norm(res_ref[...]) * (1.0 + mod_ref[1:2]) + mod_ref[0:1]).astype(BF16)
        total[...] = jnp.zeros_like(total)
    hidden = lax.dot_general(a_buf[...], w1_ref[...], (((1,), (1,)), ((), ())), preferred_element_type=F32)
    hidden = jax.nn.gelu(hidden, approximate=True).astype(BF16)
    total[...] += jnp.dot(hidden, w2_ref[...], preferred_element_type=F32)

    @pl.when(at == pl.num_programs(0) - 1)
    def _():
        out = res_ref[...] + mod_ref[2:3] * total[...].astype(BF16).astype(F32)
        out_ref[...] = out
        next_ref[...] = (layer_norm(out) * (1.0 + mod_ref[4:5]) + mod_ref[3:4]).astype(BF16)


def mlp(residual, mods, w1, w2):
    n_own, dim = residual.shape
    whole = lambda shape: pl.BlockSpec(shape, lambda at: (0, 0))
    block = pl.BlockSpec((F_ROWS, dim), lambda at: (at, 0))
    return pl.pallas_call(
        mlp_kernel,
        grid=(w1.shape[0] // F_ROWS,),
        out_shape=[jax.ShapeDtypeStruct((n_own, dim), F32), jax.ShapeDtypeStruct((n_own, dim), BF16)],
        in_specs=[whole((n_own, dim)), whole(mods.shape), block, block],
        out_specs=[whole((n_own, dim)), whole((n_own, dim))],
        scratch_shapes=[pltpu.VMEM((n_own, dim), BF16), pltpu.VMEM((n_own, dim), F32)],
        compiler_params=pltpu.CompilerParams(vmem_limit_bytes=48 << 20),
        cost_estimate=pl.CostEstimate(flops=4 * n_own * dim * w1.shape[0], bytes_accessed=4 * dim * w1.shape[0], transcendentals=0),
        name='norm_mlp',
    )(residual, mods, w1, w2)


def final_kernel(n_tp, n_cfg, n_img, eps_ref, x_ref, co_ref, out_ref, pair_buf, send_buf, pair_send, pair_recv, send_sem, recv_sem):
    me = lax.axis_index('tp')
    row = lax.axis_index('cfg')
    pair, up, down = lax.rem(row + n_img, n_cfg), lax.rem(row + 1, n_cfg), lax.rem(row + n_cfg - 1, n_cfg)
    image = lax.rem(row, n_img)
    barrier = pltpu.get_barrier_semaphore()
    pl.semaphore_signal(barrier, inc=1, device_id={'cfg': pair}, device_id_type=MESH)
    for step in range(n_tp):
        tp = lax.rem(me + step, n_tp)
        if step:
            pl.semaphore_signal(barrier, inc=1, device_id={'tp': tp}, device_id_type=MESH)
        pl.semaphore_signal(barrier, inc=1, device_id={'cfg': down, 'tp': tp}, device_id_type=MESH)
    pl.semaphore_wait(barrier, 2 * n_tp)
    swap = pltpu.make_async_remote_copy(src_ref=eps_ref, dst_ref=pair_buf, send_sem=pair_send, recv_sem=pair_recv,
                                        device_id={'cfg': pair}, device_id_type=MESH)
    swap.start()
    swap.wait()
    is_cond = row < n_img
    mine, other = eps_ref[...], pair_buf[...]
    cond, uncond = jnp.where(is_cond, mine, other), jnp.where(is_cond, other, mine)
    guided = uncond + GUIDANCE * (cond - uncond)
    x_zero = (x_ref[...] - co_ref[0:1] * guided) / co_ref[1:2]
    result = co_ref[2:3] * x_zero + co_ref[3:4] * guided
    send_buf[...] = result
    out_ref[image, me] = result

    def chunk_copy(step, ring, origin, img, dev):
        k = step * 2 + ring
        return pltpu.make_async_remote_copy(src_ref=send_buf, dst_ref=out_ref.at[img, origin], send_sem=send_sem.at[k],
                                            recv_sem=recv_sem.at[k], device_id=dev, device_id_type=MESH)

    for ring in range(2):
        for step in range(1 - ring, n_tp):
            tp = lax.rem(me + step, n_tp)
            chunk_copy(step, ring, me, image, {'cfg': up, 'tp': tp} if ring else {'tp': tp}).start()
    for ring in range(2):
        for step in range(1 - ring, n_tp):
            origin = lax.rem(me + n_tp - step, n_tp)
            img = lax.rem(down, n_img) if ring else image
            dev = {'cfg': down, 'tp': origin} if ring else {'tp': origin}
            chunk_copy(step, ring, origin, img, dev).wait_recv()
            chunk_copy(step, ring, origin, img, dev).wait_send()


def final_step(mesh, eps, x_own, coef, n_img):
    n_tp, n_cfg = mesh.shape['tp'], mesh.shape['cfg']
    vmem = pl.BlockSpec(memory_space=pltpu.VMEM)
    sem = pltpu.SemaphoreType.DMA
    return pl.pallas_call(
        functools.partial(final_kernel, n_tp, n_cfg, n_img),
        out_shape=jax.ShapeDtypeStruct((n_img, n_tp) + eps.shape, F32),
        in_specs=[vmem] * 3,
        out_specs=vmem,
        scratch_shapes=[pltpu.VMEM(eps.shape, F32), pltpu.VMEM(eps.shape, F32), sem, sem, sem((2 * n_tp,)), sem((2 * n_tp,))],
        compiler_params=pltpu.CompilerParams(collective_id=16, has_side_effects=True),
        name='guide_and_share',
    )(eps, x_own, coef)


def gather_kernel(n_tp, x_ref, out_ref, send_sem, recv_sem, loc_sem):
    me = lax.axis_index('tp')
    east, west, opp = lax.rem(me + 2, n_tp), lax.rem(me + n_tp - 2, n_tp), lax.rem(me + 4, n_tp)
    flip = lambda idx: idx + 1 - 2 * lax.rem(idx, 2)
    mate = flip(me)
    to_east, to_west, to_mate = {'tp': east}, {'tp': west}, {'tp': mate}
    half = x_ref.shape[0] // 2
    barrier = pltpu.get_barrier_semaphore()
    for dev in (to_east, to_west, to_mate):
        pl.semaphore_signal(barrier, inc=1, device_id=dev, device_id_type=MESH)
    pl.semaphore_wait(barrier, 3)
    wires = Wires(send_sem, recv_sem)
    low, high = pl.ds(0, half), pl.ds(half, half)
    for tag, cut in (('l', low), ('h', high)):
        order = (('E', to_east), ('W', to_west)) if tag == 'l' else (('W', to_west), ('E', to_east))
        for side, dev in order:
            wires.start((side, tag), x_ref.at[cut], out_ref.at[me, cut], dev)
    wires.start(('own',), x_ref, out_ref.at[me], to_mate)
    local = pltpu.make_async_copy(x_ref, out_ref.at[me], loc_sem)
    local.start()
    wires.arrived(('E', 'l'), out_ref.at[west, low], to_west)
    part = out_ref.at[west, low]
    wires.start(('fE',), part, part, to_east)
    wires.start(('d', 'wl'), part, part, to_mate)
    wires.arrived(('W', 'h'), out_ref.at[east, high], to_east)
    part = out_ref.at[east, high]
    wires.start(('fW',), part, part, to_west)
    wires.start(('d', 'eh'), part, part, to_mate)
    for key, tag, part, dev in ((('E', 'h'), 'wh', out_ref.at[west, high], to_west), (('W', 'l'), 'el', out_ref.at[east, low], to_east),
                                (('fE',), 'ol', out_ref.at[opp, low], to_west), (('fW',), 'oh', out_ref.at[opp, high], to_east)):
        wires.arrived(key, part, dev)
        wires.start(('d', tag), part, part, to_mate)
    for shard, tag in ((west, 'w'), (east, 'e'), (opp, 'o')):
        wires.arrived(('d', tag + 'l'), out_ref.at[flip(shard), low], to_mate)
        wires.arrived(('d', tag + 'h'), out_ref.at[flip(shard), high], to_mate)
    wires.arrived(('own',), out_ref.at[mate], to_mate)
    wires.drain()
    local.wait()


def gather_tokens(mesh, layer, part):
    n_tp = mesh.shape['tp']
    sem = pltpu.SemaphoreType.DMA
    return pl.pallas_call(
        functools.partial(gather_kernel, n_tp),
        out_shape=jax.ShapeDtypeStruct((n_tp,) + part.shape, BF16),
        in_specs=[pl.BlockSpec(memory_space=pltpu.VMEM)],
        out_specs=pl.BlockSpec(memory_space=pl.ANY),
        scratch_shapes=[sem((13,)), sem((13,)), sem],
        compiler_params=pltpu.CompilerParams(collective_id=8 + layer, has_side_effects=True),
        name=f'gather_tokens_{layer}',
    )(part)


def solution(mesh):
    row_spec = P(('dp', 'cfg'))
    part_spec = P('dp')
    in_specs = (row_spec, row_spec, row_spec, part_spec, part_spec, part_spec, part_spec, P(),
                P(None, None, None, 'tp'), P(None, 'tp'), P(None, None, 'tp'), P(None, None, None, 'tp'),
                P(None, 'tp'), P(None, None, 'tp'), P(None, 'tp'), P(), P(), P())
    n_tp, n_cfg = mesh.shape['tp'], mesh.shape['cfg']

    def local_step(hidden, caption, cap_len, t_block, t_embed, x_t, alpha_bar, mod_table, w_qkv, w_proj, w_cq, w_ckv, w_cproj, w_fc1, w_fc2, final_table, w_out, b_out):
        _, n_tok, dim = hidden.shape
        n_layers, n_heads, head_dim = w_proj.shape[:3]
        width = n_heads * head_dim
        n_own = n_tok // n_tp
        n_text = caption.shape[1]
        n_img = t_block.shape[0]
        image = lax.axis_index('cfg') % n_img
        me = lax.axis_index('tp')
        t_rows = lax.dynamic_index_in_dim(t_block, image, keepdims=False).astype(F32).reshape(6, dim)
        emb_row = lax.dynamic_index_in_dim(t_embed, image, keepdims=False).astype(F32)
        key_mask = (jnp.arange(n_text) < cap_len[0])[None, None, :]
        residual = lax.dynamic_slice_in_dim(hidden[0], me * n_own, n_own).astype(F32)
        all_mods = mod_table.astype(F32) + t_rows[None]
        final_mods = final_table.astype(F32) + emb_row[None, :]
        attn_in = hidden[0]
        for layer in range(n_layers):
            mods = all_mods[layer]
            if layer:
                attn_in = gather_tokens(mesh, layer, next_in).reshape(n_tok, dim)
            w_t = w_qkv[layer].transpose(1, 2, 3, 0).reshape(3, width, dim)
            kv = dot32('td,dshe->shet', caption[0], w_ckv[layer]).astype(BF16).reshape(2 * n_heads, head_dim, n_text)
            f_rows = w_fc2.shape[1] // n_cfg
            shards = (w_proj[layer].reshape(width, dim), w_cq[layer].reshape(dim, width).T, w_cproj[layer].reshape(width, dim),
                      w_fc1[layer].T.reshape(n_cfg, f_rows, dim), w_fc2[layer].reshape(n_cfg, f_rows, dim))
            o_all, kv_all, g_proj, g_cq, g_cproj, g_fc1, g_fc2 = attend_and_gather(mesh, layer, layer == 0, n_heads, attn_in, w_t, mods, kv, shards)
            self_out = dot32('kn,kd->nd', o_all.reshape(n_tp * width, n_own), g_proj.reshape(n_tp * width, dim)).astype(BF16)
            residual = residual + mods[2] * self_out.astype(F32)
            cross_q = dot32('nd,hed->hne', residual.astype(BF16), g_cq.reshape(n_tp * n_heads, head_dim, dim)).astype(BF16)
            kv_all = kv_all.reshape(n_tp, 2, n_heads, head_dim, n_text)
            cross_k = kv_all[:, 0].reshape(n_tp * n_heads, head_dim, n_text)
            cross_v = kv_all[:, 1].reshape(n_tp * n_heads, head_dim, n_text)
            scores = dot32('hne,het->hnt', cross_q, cross_k) * head_dim ** -0.5
            scores = jnp.where(key_mask, scores, -1e30)
            probs = jax.nn.softmax(scores, axis=-1).astype(BF16)
            cross_o = dot32('hnt,het->nhe', probs, cross_v).astype(BF16)
            cross_out = dot32('nk,kd->nd', cross_o.reshape(n_own, n_tp * width), g_cproj.reshape(n_tp * width, dim)).astype(BF16)
            residual = residual + cross_out.astype(F32)
            after = all_mods[layer + 1, :2] if layer + 1 < n_layers else final_mods
            mlp_mods = jnp.concatenate([mods[3:6], after, jnp.zeros((3, dim), F32)], axis=0)
            n_ff = g_fc1.shape[0] * g_fc1.shape[1] * g_fc1.shape[2]
            residual, next_in = mlp(residual, mlp_mods, g_fc1.reshape(n_ff, dim), g_fc2.reshape(n_ff, dim))
        side = x_t.shape[1]
        grid = side // 2
        n_own_rows = n_own // grid
        out_tok = dot32('nd,dc->cn', next_in, w_out) + b_out.astype(F32)[:, None]
        eps = out_tok.reshape(2, 2, 8, n_own_rows, grid)[:, :, :4]
        place = (jnp.arange(side)[None, None, :] == 2 * jnp.arange(grid)[None, :, None] + jnp.arange(2)[:, None, None]).astype(F32)
        eps = jnp.einsum('pqcij,qjx->ipcx', eps, place, precision=lax.Precision.HIGHEST, preferred_element_type=F32)
        eps = eps.reshape(n_own_rows * 2 * 4, side)
        x_rows = x_t.transpose(0, 1, 3, 2).reshape(n_img, n_tp, n_own_rows * 2 * 4, side)
        x_own = lax.dynamic_slice(x_rows, (image, me, 0, 0), (1, 1) + x_rows.shape[2:])[0, 0]
        abar = lax.dynamic_index_in_dim(alpha_bar, image, keepdims=False)
        coef = jnp.stack([jnp.sqrt(1.0 - abar[0]), jnp.sqrt(abar[0]), jnp.sqrt(abar[1]), jnp.sqrt(1.0 - abar[1])])
        coef = jnp.broadcast_to(jnp.concatenate([coef, coef])[:, None], (8, side))
        x_prev = final_step(mesh, eps, x_own, coef, n_img)
        return x_prev.reshape(n_img, side, 4, side).transpose(0, 1, 3, 2)

    return jax.shard_map(local_step, mesh=mesh, in_specs=in_specs, out_specs=part_spec, check_vma=False)
```

time: 1160 us -> 356 us (0.31)
  waiting for transfers between devices: 671 us -> 0 us
  matrix products: 333 us -> 32.3 us
  Pallas kernels: 0 us -> 283 us
  other arithmetic: 115 us -> 9.87 us
    psum x6 -> x0, waiting for transfers between devices: 652 us -> none  [the longest x2 218 us: tp_block(): lax.psum(self_part, 'tp').astype(jnp.float32)]
    pallas_call x0 -> x6, Pallas kernels: none -> 283 us  [the longest x2 179 us: attend_and_gather(): pl.pallas_call(functools.partial(attn_kernel, n_tp, n_cfg, head_dim, head...]
    dot_general x9 -> x12, matrix products: 170 us -> 32.3 us  [the longest x11 32.1 us: dot32(): return jnp.einsum(spec, left, right, preferred_element_type=F32)]
    sub x4 -> x0, matrix products: 122 us -> none  [attention(): attn_prob = jax.nn.softmax(scores, axis=-1).astype(jnp.bfloat16)]
    reduce_sum x10 -> x0, other arithmetic: 108 us -> none  [the longest x5 68.7 us: layer_norm(): mean_val = jnp.mean(values, axis=-1, keepdims=True)]
    unnamed x6 -> x0, matrix products: 41.2 us -> none
    all_gather x1 -> x0, waiting for transfers between devices: 19.2 us -> none  [local_step(): eps_all = lax.all_gather(eps_local, 'cfg', axis=0, tiled=True)]
  transfers between devices with their start and end apart: 7 -> 0, of which waited for: 7 -> 0; matrix products, arithmetic and copies ran while one was open for 0% -> 0% of each run, Pallas kernels for 0% -> 0%
where the time goes in v1:
time: 356 us; the launch traced here: 349 us
  Pallas kernels  283 us (79%)
  matrix products  32.3 us (9%)
  local copies, waits for them, and re-layouts  19.8 us (6%)
  other arithmetic  9.87 us (3%)
  between operations  4.02 us (1%)
    pallas_call x2, Pallas kernels, attend_and_gather(): pl.pallas_call(functools.partial(attn_kernel, n_tp, n_cfg, head_dim, head...  179 us
    pallas_call x1, Pallas kernels, gather_tokens(): pl.pallas_call(functools.partial(gather_kernel, n_tp), out_shape=jax.Shap...  46.1 us
    pallas_call x2, Pallas kernels, mlp(): pl.pallas_call(mlp_kernel, grid=(w1.shape[0] // F_ROWS,), out_shape=[jax....  42 us
    dot_general x11, matrix products, dot32(): return jnp.einsum(spec, left, right, preferred_element_type=F32)  32.1 us
    pallas_call x1, Pallas kernels, final_step(): pl.pallas_call(functools.partial(final_kernel, n_tp, n_cfg, n_img), out_s...  15.6 us
    sub x2, other arithmetic, local_step(): probs = jax.nn.softmax(scores, axis=-1).astype(BF16)  9.64 us

profile of v1, /device:TPU:97, one launch (start us, length us, event | category | flops | bytes accessed | tf_op | source)
XLA Modules:
  0.0 348.7 jit_solution(3164319554616869535)
XLA Ops:
  0.0 0.0 copy-start.17
  0.0 3.1 fusion.53
  3.1 0.1 convert_reduce_fusion
  3.3 0.6 slice_bitcast_fusion
  3.9 2.2 convolution_convert_fusion.5
  6.1 0.0 copy-done.7
  6.1 0.9 fusion.56
  7.0 0.9 fusion.55
  7.9 0.0 copy-done.9
  7.9 0.9 fusion.54
  8.9 1.7 fusion.52
  10.5 1.0 copy-done.4
  11.6 1.7 fusion.51
  13.2 93.1 %attend_gather_0.1 = (bf16[8,144,512]{2,1,0:T(8,128)(2,1)}, bf16[8,4,72,120]{3,2,1,0:T(8,128)(2,1)}, bf16[8,144,1152]{2,1,0:T(8,128)(2,1)}, bf16[8,144,1152]{2,1...) custom-call(bf16[4096,1152]{1,0:T(8,128)(2,1)} %bitcast.161, ...), custom_call_target="tpu_custom_call" | custom-call | tf_op jit(solution)/shard_map/attend_gather_0/pallas_call | solution.py:260
  106.4 4.4 %fusion.7 = f32[512,1152]{1,0:T(8,128)S(1)} fusion(bf16[8,144,512]{2,1,0:T(8,128)(2,1)} %get-tuple-element.22, bf16[8,144,1152]{2,1,0:T(8,128)(2,1)} %get-tuple-element.23, f32[1152]{0:T(1024)S(1)} %get-tuple-element.40, bf16[1,4096,1152]{2,1,0:T(8,128)(2,1)} %param.18, s32[]{:T(128)S(6)} %select_n.29), kind=kOutput, calls=%fused_computation.15 | convolution fusion | flops 1361903616 | bytes 7377412 | tf_op jit(solution)/shard_map/kn,kd->nd/dot_general | solution.py:28
  110.9 5.9 %fusion.27 = f32[16,512,120]{1,2,0:T(8,128)} fusion(bf16[16,72,120]{2,1,0:T(8,128)(2,1)S(1)} %bitcast.179, bf16[16,72,1152]{2,1,0:T(8,128)(2,1)} %bitcast.169, f32[512,1152]{1,0:T(8,128)S(1)} %fusion.7), kind=kOutput, calls=%fused_computation.39 | convolution fusion | flops 1501691904 | bytes 9222144 | tf_op jit(solution)/shard_map/hne,het->hnt/dot_general | solution.py:28
  117.5 4.8 %fusion.60 = (f32[16,512]{1,0:T(8,128)S(1)}, f32[16,512,120]{1,2,0:T(8,128)S(1)}) fusion(f32[16,512,120]{1,2,0:T(8,128)} %fusion.27, pred[120]{0:T(512)(128)(4,1)S(1)} %iota_compare_fusion.1), kind=kOutput, calls=%fused_computation.90 | output fusion | flops 5898359 | bytes 7897208 | tf_op jit(solution)/shard_map/sub | solution.py:463
  122.3 0.6 fusion.25
  122.9 1.2 copy-done.5
  124.1 1.9 fusion.15.res_ref
  126.0 0.1 pad.5.clone
  126.1 0.1 maximum_maximum_fusion.1
  126.2 20.4 %norm_mlp.2 = (f32[512,1152]{1,0:T(8,128)S(1)}, bf16[512,1152]{1,0:T(8,128)(2,1)S(1)}) custom-call(f32[512,1152]{1,0:T(8,128)S(1)} %fusion.15.res_ref, f32[8,1152]{1,0:T(8,128)S(1)} %get-tuple-element.64.mod_ref, bf16[4608,1152]{1,0:T(8,128)(2,1)} %bitcast.190, bf16[4608,1152]{1,0:T(8,128)(2,1)} %bitcast.191), custom_call_target="tpu_custom_call" | custom-call | flops 10871635968 | bytes 21233664 | tf_op jit(solution)/shard_map/norm_mlp/pallas_call | solution.py:295
  146.6 1.0 copy-done.1
  147.6 46.1 %gather_tokens_1.1 = bf16[8,512,1152]{2,1,0:T(8,128)(2,1)} custom-call(bf16[512,1152]{1,0:T(8,128)(2,1)} %copy-done.1), custom_call_target="tpu_custom_call" | custom-call | tf_op jit(solution)/shard_map/gather_tokens_1/pallas_call | solution.py:410
  193.7 2.1 convolution_convert_fusion.4
  195.8 86.0 %attend_gather_1.1 = (bf16[8,144,512]{2,1,0:T(8,128)(2,1)}, bf16[8,4,72,120]{3,2,1,0:T(8,128)(2,1)}, bf16[8,144,1152]{2,1,0:T(8,128)(2,1)}, bf16[8,144,1152]{2,1...) custom-call(bf16[4096,1152]{1,0:T(8,128)(2,1)} %bitcast.160, ...), custom_call_target="tpu_custom_call" | custom-call | tf_op jit(solution)/shard_map/attend_gather_1/pallas_call | solution.py:260
  281.8 5.6 %fusion.11 = f32[512,1152]{1,0:T(8,128)} fusion(f32[512,1152]{1,0:T(8,128)S(1)} %get-tuple-element.29, bf16[8,144,512]{2,1,0:T(8,128)(2,1)} %get-tuple-element.31, bf16[8,144,1152]{2,1,0:T(8,128)(2,1)} %get-tuple-element.32, f32[1152]{0:T(1024)S(1)} %get-tuple-element.39), kind=kOutput, calls=%fused_computation.19 | convolution fusion | flops 1361313792 | bytes 8557056 | tf_op jit(solution)/shard_map/kn,kd->nd/dot_general | solution.py:28
  287.4 6.6 %fusion.26 = f32[16,512,120]{1,2,0:T(8,128)} fusion(bf16[16,72,120]{2,1,0:T(8,128)(2,1)S(1)} %bitcast.180, bf16[16,72,1152]{2,1,0:T(8,128)(2,1)} %bitcast.171, f32[512,1152]{1,0:T(8,128)} %fusion.11), kind=kOutput, calls=%fused_computation.37 | convolution fusion | flops 1501691904 | bytes 9222144 | tf_op jit(solution)/shard_map/hne,het->hnt/dot_general | solution.py:28
  294.1 4.8 %fusion.61 = (f32[16,512]{1,0:T(8,128)S(1)}, f32[16,512,120]{1,2,0:T(8,128)S(1)}) fusion(f32[16,512,120]{1,2,0:T(8,128)} %fusion.26, pred[120]{0:T(512)(128)(4,1)S(1)} %copy-done.22), kind=kOutput, calls=%fused_computation.91 | output fusion | flops 5898359 | bytes 7897208 | tf_op jit(solution)/shard_map/sub | solution.py:463
  298.9 0.6 fusion.24
  299.5 1.1 copy-done.2
  300.6 0.8 copy-done.6
  301.4 1.9 fusion.13.res_ref
  303.2 0.0 copy-start.20
  303.3 0.0 copy-start.12
  303.3 0.0 copy-start.19
  303.3 21.6 %norm_mlp.3 = (f32[512,1152]{1,0:T(8,128)}, bf16[512,1152]{1,0:T(8,128)(2,1)S(1)}) custom-call(f32[512,1152]{1,0:T(8,128)S(1)} %fusion.13.res_ref, f32[8,1152]{1,0:T(8,128)S(1)} %get-tuple-element.63.mod_ref, bf16[4608,1152]{1,0:T(8,128)(2,1)} %bitcast.192, bf16[4608,1152]{1,0:T(8,128)(2,1)} %bitcast.193), custom_call_target="tpu_custom_call" | custom-call | flops 10871635968 | bytes 21233664 | tf_op jit(solution)/shard_map/norm_mlp/pallas_call | solution.py:295
  324.9 0.4 fusion.36
  325.3 0.1 reshape.162
  325.5 0.2 convolution_bitcast_fusion.2
  325.7 0.6 copy.21
  326.3 0.6 dynamic-slice_bitcast_fusion.x_ref
  326.9 0.6 fusion.59
  330.1 0.1 concatenate.12
  330.2 0.7 broadcast_in_dim.20.co_ref
  330.8 15.6 %guide_and_share.1 = f32[2,8,64,128]{3,2,1,0:T(8,128)} custom-call(f32[64,128]{1,0:T(8,128)} %bitcast.187, f32[64,128]{1,0:T(8,128)} %dynamic-slice_bitcast_fusion.x_ref, f32[8,128]{1,0:T(8,128)} %broadcast_in_dim.20.co_ref), custom_call_target="tpu_custom_call" | custom-call | tf_op jit(solution)/shard_map/guide_and_share/pallas_call | solution.py:356
  346.4 1.9 copy.29
  (50 shorter events, 0.3 us)
Async XLA Ops:
  0.0 326.3 %copy-start = (f32[2,128,128,4]{2,3,1,0:T(4,128)S(1)}, f32[2,128,128,4]{2,3,1,0:T(4,128)}, u32[]{:S(2)}) copy-start(f32[2,128,128,4]{2,3,1,0:T(4,128)} %param.23) | copy-start | bytes 1572868
  0.0 3.2 copy-start.14
  0.0 3.1 copy-start.13
  0.0 3.9 %copy-start.17 = (bf16[1,120,1152]{2,1,0:T(8,128)(2,1)S(1)}, bf16[1,120,1152]{2,1,0:T(8,128)(2,1)}, u32[]{:S(2)}) copy-start(bf16[1,120,1152]{2,1,0:T(8,128)(2,1)} %param.19) | copy-start | bytes 829444
  0.0 6.1 %copy-start.7 = (bf16[2,2,72,1152]{3,2,1,0:T(8,128)(2,1)S(1)}, bf16[2,2,72,1152]{3,2,1,0:T(8,128)(2,1)}, u32[]{:S(2)}) copy-start(bf16[2,2,72,1152]{3,2,1,0:T(8,128)(2,1)} %param.27) | copy-start | bytes 1990660
  3.1 3.9 %copy-start.8 = (bf16[2,1152,2,72]{1,3,2,0:T(8,128)(2,1)S(1)}, bf16[2,1152,2,72]{1,3,2,0:T(8,128)(2,1)}, u32[]{:S(2)}) copy-start(bf16[2,1152,2,72]{1,3,2,0:T(8,128)(2,1)} %param.28) | copy-start | bytes 1990660
  3.1 4.8 %copy-start.9 = (bf16[2,2,72,1152]{3,2,1,0:T(8,128)(2,1)S(1)}, bf16[2,2,72,1152]{3,2,1,0:T(8,128)(2,1)}, u32[]{:S(2)}) copy-start(bf16[2,2,72,1152]{3,2,1,0:T(8,128)(2,1)} %param.30) | copy-start | bytes 1990660
  3.9 4.9 %copy-start.3 = (bf16[2,1152,576]{1,2,0:T(8,128)(2,1)S(1)}, bf16[2,1152,576]{1,2,0:T(8,128)(2,1)}, u32[]{:S(2)}) copy-start(bf16[2,1152,576]{1,2,0:T(8,128)(2,1)} %param.31) | copy-start | bytes 7962628
  8.9 2.7 copy-start.4
  106.4 4.4 %copy-start.10 = (bf16[8,4,72,120]{3,2,1,0:T(8,128)(2,1)S(1)}, bf16[8,4,72,120]{3,2,1,0:T(8,128)(2,1)}, u32[]{:S(2)}) copy-start(bf16[8,4,72,120]{3,2,1,0:T(8,128)(2,1)} %get-tuple-element.24) | copy-start | bytes 1658884
  117.4 4.8 %copy-start.21 = (pred[120]{0:T(512)(128)(4,1)}, pred[120]{0:T(512)(128)(4,1)S(1)}, u32[]{:S(2)}) copy-start(pred[120]{0:T(512)(128)(4,1)S(1)} %iota_compare_fusion.1) | copy-start | bytes 364
  122.3 1.8 copy-start.5
  124.1 1.9 copy-start.15
  124.1 1.9 copy-start.16
  146.6 1.0 copy-start.1
  147.6 46.1 %copy-start.18 = (bf16[1,120,1152]{2,1,0:T(8,128)(2,1)S(1)}, bf16[1,120,1152]{2,1,0:T(8,128)(2,1)}, u32[]{:S(2)}) copy-start(bf16[1,120,1152]{2,1,0:T(8,128)(2,1)} %param.19) | copy-start | bytes 829444
  281.8 5.6 %copy-start.11 = (bf16[8,4,72,120]{3,2,1,0:T(8,128)(2,1)S(1)}, bf16[8,4,72,120]{3,2,1,0:T(8,128)(2,1)}, u32[]{:S(2)}) copy-start(bf16[8,4,72,120]{3,2,1,0:T(8,128)(2,1)} %get-tuple-element.33) | copy-start | bytes 1658884
  287.4 6.6 %copy-start.22 = (pred[120]{0:T(512)(128)(4,1)S(1)}, pred[120]{0:T(512)(128)(4,1)}, u32[]{:S(2)}) copy-start(pred[120]{0:T(512)(128)(4,1)} %copy-done.21) | copy-start | bytes 364
  298.9 1.7 copy-start.2
  298.9 2.5 copy-start.6
  303.2 21.6 %copy-start.20 = (bf16[32]{0:T(256)(128)(2,1)S(1)}, bf16[32]{0:T(256)(128)(2,1)}, u32[]{:S(2)}) copy-start(bf16[32]{0:T(256)(128)(2,1)} %param.35) | copy-start | bytes 196
  303.3 21.6 %copy-start.12 = (bf16[1152,32]{0,1:T(8,128)(2,1)S(1)}, bf16[1152,32]{0,1:T(8,128)(2,1)}, u32[]{:S(2)}) copy-start(bf16[1152,32]{0,1:T(8,128)(2,1)} %param.34) | copy-start | bytes 221188
  303.3 23.7 %copy-start.19 = (f32[2,2]{1,0:T(2,128)S(1)}, f32[2,2]{1,0:T(2,128)}, u32[]{:S(2)}) copy-start(f32[2,2]{1,0:T(2,128)} %param.24) | copy-start | bytes 52

commit v2 on v1

--- a/solution.py
+++ b/solution.py
@@ -14,7 +14,8 @@
 BF16 = jnp.bfloat16
 F32 = jnp.float32
 K_ROWS = 512
-F_ROWS = 768
+SPAN = 4
+F_ROWS = 512
 
 
 def layer_norm(values):
@@ -163,11 +164,10 @@
     loads = [pltpu.make_async_copy(a_in.at[pl.ds(i * chunk_rows, chunk_rows)], a_buf.at[i], a_sem.at[i]) for i in range(n_chunk)]
     for load in loads:
         load.start()
-    for load in loads:
-        load.wait()
     v_ref[:, head_dim:] = jnp.ones((n_heads, v_ref.shape[1] - head_dim, v_ref.shape[2]), BF16)
 
     def project(at, carry):
+        pltpu.make_async_copy(a_in.at[pl.ds(at * chunk_rows, chunk_rows)], a_buf.at[at], a_sem.at[at]).wait()
         act = a_buf[at]
         if norm:
             act = (layer_norm(act.astype(F32)) * (1.0 + mod_ref[1:2]) + mod_ref[0:1]).astype(BF16)
@@ -179,7 +179,7 @@
         for h in range(n_heads):
             v_ref[h, :head_dim, cols] = vals[h * head_dim:(h + 1) * head_dim]
         if norm:
-            pl.when(at == 5)(lambda: ev_x_near('fc1'))
+            pl.when(at == 3)(lambda: ev_x_near('fc1'))
         return carry
 
     lax.fori_loop(0, n_chunk, project, 0)
@@ -195,21 +195,25 @@
         chunk = lax.rem(me + 1 + step, n_tp)
         q_all = q_ref[:, pl.ds(pl.multiple_of(chunk * chunk_rows, chunk_rows), chunk_rows)]
         queries = [jnp.where((row_ids >= h * head_dim) & (row_ids < (h + 1) * head_dim), q_all, 0) for h in range(n_heads)]
-        units = [(h, j) for j in range(k_ref.shape[0] // K_ROWS) for h in range(n_heads)]
-        score = lambda unit: jnp.dot(k_ref[pl.ds(unit[1] * K_ROWS, K_ROWS)], queries[unit[0]], preferred_element_type=F32)
-        top, mixed = [None] * n_heads, [None] * n_heads
-        scores = score(units[0])
-        for at, (h, j) in enumerate(units):
-            ahead = score(units[at + 1]) if at + 1 < len(units) else None
-            peak = jnp.max(scores, axis=0, keepdims=True)
-            if j:
-                peak = jnp.maximum(peak, top[h])
+        units = [(h, j) for j in range(SPAN) for h in range(n_heads)]
+
+        def span(turn, state):
+            top, mixed = list(state[:n_heads]), list(state[n_heads:])
+            rows = lambda j: pl.ds(pl.multiple_of((turn * SPAN + j) * K_ROWS, K_ROWS), K_ROWS)
+            score = lambda unit: jnp.dot(k_ref[rows(unit[1])], queries[unit[0]], preferred_element_type=F32)
+            scores = score(units[0])
+            for at, (h, j) in enumerate(units):
+                ahead = score(units[at + 1]) if at + 1 < len(units) else None
+                peak = jnp.maximum(jnp.max(scores, axis=0, keepdims=True), top[h])
                 fade = jnp.exp2((top[h] - peak) * (scale * LOG2E))
-            top[h] = peak
-            probs = jnp.exp2((scores - peak) * (scale * LOG2E)).astype(BF16)
-            term = jnp.dot(v_ref[h, :, pl.ds(j * K_ROWS, K_ROWS)], probs, preferred_element_type=F32)
-            mixed[h] = mixed[h] * fade + term if j else term
-            scores = ahead
+                top[h] = peak
+                probs = jnp.exp2((scores - peak) * (scale * LOG2E)).astype(BF16)
+                mixed[h] = mixed[h] * fade + jnp.dot(v_ref[h, :, rows(j)], probs, preferred_element_type=F32)
+                scores = ahead
+            return (*top, *mixed)
+
+        state = [jnp.full((1, chunk_rows), -jnp.inf, F32)] * n_heads + [jnp.zeros((v_ref.shape[1], chunk_rows), F32)] * n_heads
+        mixed = lax.fori_loop(0, k_ref.shape[0] // (K_ROWS * SPAN), span, tuple(state))[n_heads:]
         outs = [part[:head_dim] / part[head_dim:head_dim + 1] for part in mixed]
         o_buf[step] = jnp.concatenate(outs, axis=0).astype(BF16)
 

time: 356 us -> 341 us (0.958); the launches traced: 349 us -> 341 us
  Pallas kernels: 283 us -> 275 us
    pallas_call x2, Pallas kernels: 179 us -> 173 us  [attend_and_gather(): pl.pallas_call(functools.partial(attn_kernel, n_tp, n_cfg, head_dim, head...]
where the time goes in v2:
time: 341 us
  Pallas kernels  275 us (81%)
  matrix products  32.3 us (9%)
  local copies, waits for them, and re-layouts  19.8 us (6%)
  other arithmetic  9.87 us (3%)
  between operations  3.58 us (1%)
    pallas_call x2, Pallas kernels, attend_and_gather(): pl.pallas_call(functools.partial(attn_kernel, n_tp, n_cfg, head_dim, head...  173 us
    pallas_call x1, Pallas kernels, gather_tokens(): pl.pallas_call(functools.partial(gather_kernel, n_tp), out_shape=jax.Shap...  46.1 us
    pallas_call x2, Pallas kernels, mlp(): pl.pallas_call(mlp_kernel, grid=(w1.shape[0] // F_ROWS,), out_shape=[jax....  39.7 us
    dot_general x11, matrix products, dot32(): return jnp.einsum(spec, left, right, preferred_element_type=F32)  32.1 us
    pallas_call x1, Pallas kernels, final_step(): pl.pallas_call(functools.partial(final_kernel, n_tp, n_cfg, n_img), out_s...  16.4 us
    sub x2, other arithmetic, local_step(): probs = jax.nn.softmax(scores, axis=-1).astype(BF16)  9.64 us
    unnamed x47, local copies, waits for them, and re-layouts  7.07 us

profile of v2, /device:TPU:97, one launch (start us, length us, event | category | flops | bytes accessed | tf_op | source)
XLA Modules:
  0.0 340.9 jit_solution(3522472399634114321)
XLA Ops:
  0.0 0.0 copy-start
  0.0 0.0 copy-start.17
  0.0 3.1 fusion.53
  3.1 0.1 convert_reduce_fusion
  3.2 0.0 copy-done.14
  3.3 0.6 slice_bitcast_fusion
  3.9 2.2 convolution_convert_fusion.5
  6.1 0.9 fusion.56
  7.0 0.9 fusion.55
  7.9 0.9 fusion.54
  8.9 1.7 fusion.52
  10.5 1.0 copy-done.4
  11.6 1.7 fusion.51
  13.2 88.4 %attend_gather_0.1 = (bf16[8,144,512]{2,1,0:T(8,128)(2,1)}, bf16[8,4,72,120]{3,2,1,0:T(8,128)(2,1)}, bf16[8,144,1152]{2,1,0:T(8,128)(2,1)}, bf16[8,144,1152]{2,1...) custom-call(bf16[4096,1152]{1,0:T(8,128)(2,1)} %bitcast.161, ...), custom_call_target="tpu_custom_call" | custom-call | tf_op jit(solution)/shard_map/attend_gather_0/pallas_call | solution.py:264
  101.7 4.4 %fusion.7 = f32[512,1152]{1,0:T(8,128)S(1)} fusion(bf16[8,144,512]{2,1,0:T(8,128)(2,1)} %get-tuple-element.22, bf16[8,144,1152]{2,1,0:T(8,128)(2,1)} %get-tuple-element.23, f32[1152]{0:T(1024)S(1)} %get-tuple-element.40, bf16[1,4096,1152]{2,1,0:T(8,128)(2,1)} %param.18, s32[]{:T(128)S(6)} %select_n.29), kind=kOutput, calls=%fused_computation.15 | convolution fusion | flops 1361903616 | bytes 7377412 | tf_op jit(solution)/shard_map/kn,kd->nd/dot_general | solution.py:29
  106.2 5.9 %fusion.27 = f32[16,512,120]{1,2,0:T(8,128)} fusion(bf16[16,72,120]{2,1,0:T(8,128)(2,1)S(1)} %bitcast.179, bf16[16,72,1152]{2,1,0:T(8,128)(2,1)} %bitcast.169, f32[512,1152]{1,0:T(8,128)S(1)} %fusion.7), kind=kOutput, calls=%fused_computation.39 | convolution fusion | flops 1501691904 | bytes 9222144 | tf_op jit(solution)/shard_map/hne,het->hnt/dot_general | solution.py:29
  112.8 4.8 %fusion.60 = (f32[16,512]{1,0:T(8,128)S(1)}, f32[16,512,120]{1,2,0:T(8,128)S(1)}) fusion(f32[16,512,120]{1,2,0:T(8,128)} %fusion.27, pred[120]{0:T(512)(128)(4,1)S(1)} %iota_compare_fusion.1), kind=kOutput, calls=%fused_computation.90 | output fusion | flops 5898359 | bytes 7897208 | tf_op jit(solution)/shard_map/sub | solution.py:467
  117.6 0.6 fusion.25
  118.2 1.2 copy-done.5
  119.4 1.9 fusion.15.res_ref
  121.3 0.1 pad.5.clone
  121.4 0.1 maximum_maximum_fusion.1
  121.5 19.2 %norm_mlp.2 = (f32[512,1152]{1,0:T(8,128)S(1)}, bf16[512,1152]{1,0:T(8,128)(2,1)S(1)}) custom-call(f32[512,1152]{1,0:T(8,128)S(1)} %fusion.15.res_ref, f32[8,1152]{1,0:T(8,128)S(1)} %get-tuple-element.64.mod_ref, bf16[4608,1152]{1,0:T(8,128)(2,1)} %bitcast.190, bf16[4608,1152]{1,0:T(8,128)(2,1)} %bitcast.191), custom_call_target="tpu_custom_call" | custom-call | flops 10871635968 | bytes 21233664 | tf_op jit(solution)/shard_map/norm_mlp/pallas_call | solution.py:299
  140.7 1.0 copy-done.1
  141.7 46.1 %gather_tokens_1.1 = bf16[8,512,1152]{2,1,0:T(8,128)(2,1)} custom-call(bf16[512,1152]{1,0:T(8,128)(2,1)} %copy-done.1), custom_call_target="tpu_custom_call" | custom-call | tf_op jit(solution)/shard_map/gather_tokens_1/pallas_call | solution.py:414
  187.8 2.1 convolution_convert_fusion.4
  189.9 84.8 %attend_gather_1.1 = (bf16[8,144,512]{2,1,0:T(8,128)(2,1)}, bf16[8,4,72,120]{3,2,1,0:T(8,128)(2,1)}, bf16[8,144,1152]{2,1,0:T(8,128)(2,1)}, bf16[8,144,1152]{2,1...) custom-call(bf16[4096,1152]{1,0:T(8,128)(2,1)} %bitcast.160, ...), custom_call_target="tpu_custom_call" | custom-call | tf_op jit(solution)/shard_map/attend_gather_1/pallas_call | solution.py:264
  274.7 5.6 %fusion.11 = f32[512,1152]{1,0:T(8,128)} fusion(f32[512,1152]{1,0:T(8,128)S(1)} %get-tuple-element.29, bf16[8,144,512]{2,1,0:T(8,128)(2,1)} %get-tuple-element.31, bf16[8,144,1152]{2,1,0:T(8,128)(2,1)} %get-tuple-element.32, f32[1152]{0:T(1024)S(1)} %get-tuple-element.39), kind=kOutput, calls=%fused_computation.19 | convolution fusion | flops 1361313792 | bytes 8557056 | tf_op jit(solution)/shard_map/kn,kd->nd/dot_general | solution.py:29
  280.4 6.6 %fusion.26 = f32[16,512,120]{1,2,0:T(8,128)} fusion(bf16[16,72,120]{2,1,0:T(8,128)(2,1)S(1)} %bitcast.180, bf16[16,72,1152]{2,1,0:T(8,128)(2,1)} %bitcast.171, f32[512,1152]{1,0:T(8,128)} %fusion.11), kind=kOutput, calls=%fused_computation.37 | convolution fusion | flops 1501691904 | bytes 9222144 | tf_op jit(solution)/shard_map/hne,het->hnt/dot_general | solution.py:29
  287.0 4.8 %fusion.61 = (f32[16,512]{1,0:T(8,128)S(1)}, f32[16,512,120]{1,2,0:T(8,128)S(1)}) fusion(f32[16,512,120]{1,2,0:T(8,128)} %fusion.26, pred[120]{0:T(512)(128)(4,1)S(1)} %copy-done.22), kind=kOutput, calls=%fused_computation.91 | output fusion | flops 5898359 | bytes 7897208 | tf_op jit(solution)/shard_map/sub | solution.py:467
  291.8 0.6 fusion.24
  292.4 1.1 copy-done.2
  293.5 0.8 copy-done.6
  294.3 1.9 fusion.13.res_ref
  296.2 0.0 copy-start.20
  296.2 0.0 copy-start.12
  296.2 0.0 copy-start.19
  296.2 20.5 %norm_mlp.3 = (f32[512,1152]{1,0:T(8,128)}, bf16[512,1152]{1,0:T(8,128)(2,1)S(1)}) custom-call(f32[512,1152]{1,0:T(8,128)S(1)} %fusion.13.res_ref, f32[8,1152]{1,0:T(8,128)S(1)} %get-tuple-element.63.mod_ref, bf16[4608,1152]{1,0:T(8,128)(2,1)} %bitcast.192, bf16[4608,1152]{1,0:T(8,128)(2,1)} %bitcast.193), custom_call_target="tpu_custom_call" | custom-call | flops 10871635968 | bytes 21233664 | tf_op jit(solution)/shard_map/norm_mlp/pallas_call | solution.py:299
  316.7 0.4 fusion.36
  317.1 0.1 reshape.162
  317.2 0.2 convolution_bitcast_fusion.2
  317.5 0.6 copy.21
  318.1 0.6 dynamic-slice_bitcast_fusion.x_ref
  318.7 0.6 fusion.59
  321.8 0.1 concatenate.12
  321.9 0.7 broadcast_in_dim.20.co_ref
  322.6 16.4 %guide_and_share.1 = f32[2,8,64,128]{3,2,1,0:T(8,128)} custom-call(f32[64,128]{1,0:T(8,128)} %bitcast.187, f32[64,128]{1,0:T(8,128)} %dynamic-slice_bitcast_fusion.x_ref, f32[8,128]{1,0:T(8,128)} %broadcast_in_dim.20.co_ref), custom_call_target="tpu_custom_call" | custom-call | tf_op jit(solution)/shard_map/guide_and_share/pallas_call | solution.py:360
  339.1 1.9 copy.29
  (50 shorter events, 0.3 us)
Async XLA Ops:
  0.0 318.1 %copy-start = (f32[2,128,128,4]{2,3,1,0:T(4,128)S(1)}, f32[2,128,128,4]{2,3,1,0:T(4,128)}, u32[]{:S(2)}) copy-start(f32[2,128,128,4]{2,3,1,0:T(4,128)} %param.23) | copy-start | bytes 1572868
  0.0 3.2 copy-start.14
  0.0 3.1 copy-start.13
  0.0 3.9 %copy-start.17 = (bf16[1,120,1152]{2,1,0:T(8,128)(2,1)S(1)}, bf16[1,120,1152]{2,1,0:T(8,128)(2,1)}, u32[]{:S(2)}) copy-start(bf16[1,120,1152]{2,1,0:T(8,128)(2,1)} %param.19) | copy-start | bytes 829444
  0.0 6.1 %copy-start.7 = (bf16[2,2,72,1152]{3,2,1,0:T(8,128)(2,1)S(1)}, bf16[2,2,72,1152]{3,2,1,0:T(8,128)(2,1)}, u32[]{:S(2)}) copy-start(bf16[2,2,72,1152]{3,2,1,0:T(8,128)(2,1)} %param.27) | copy-start | bytes 1990660
  3.1 3.9 %copy-start.8 = (bf16[2,1152,2,72]{1,3,2,0:T(8,128)(2,1)S(1)}, bf16[2,1152,2,72]{1,3,2,0:T(8,128)(2,1)}, u32[]{:S(2)}) copy-start(bf16[2,1152,2,72]{1,3,2,0:T(8,128)(2,1)} %param.28) | copy-start | bytes 1990660
  3.1 4.8 %copy-start.9 = (bf16[2,2,72,1152]{3,2,1,0:T(8,128)(2,1)S(1)}, bf16[2,2,72,1152]{3,2,1,0:T(8,128)(2,1)}, u32[]{:S(2)}) copy-start(bf16[2,2,72,1152]{3,2,1,0:T(8,128)(2,1)} %param.30) | copy-start | bytes 1990660
  3.9 4.9 %copy-start.3 = (bf16[2,1152,576]{1,2,0:T(8,128)(2,1)S(1)}, bf16[2,1152,576]{1,2,0:T(8,128)(2,1)}, u32[]{:S(2)}) copy-start(bf16[2,1152,576]{1,2,0:T(8,128)(2,1)} %param.31) | copy-start | bytes 7962628
  8.9 2.7 copy-start.4
  101.7 4.4 %copy-start.10 = (bf16[8,4,72,120]{3,2,1,0:T(8,128)(2,1)S(1)}, bf16[8,4,72,120]{3,2,1,0:T(8,128)(2,1)}, u32[]{:S(2)}) copy-start(bf16[8,4,72,120]{3,2,1,0:T(8,128)(2,1)} %get-tuple-element.24) | copy-start | bytes 1658884
  112.7 4.8 %copy-start.21 = (pred[120]{0:T(512)(128)(4,1)}, pred[120]{0:T(512)(128)(4,1)S(1)}, u32[]{:S(2)}) copy-start(pred[120]{0:T(512)(128)(4,1)S(1)} %iota_compare_fusion.1) | copy-start | bytes 364
  117.6 1.8 copy-start.5
  119.3 1.9 copy-start.15
  119.3 1.9 copy-start.16
  140.7 1.0 copy-start.1
  141.7 46.1 %copy-start.18 = (bf16[1,120,1152]{2,1,0:T(8,128)(2,1)S(1)}, bf16[1,120,1152]{2,1,0:T(8,128)(2,1)}, u32[]{:S(2)}) copy-start(bf16[1,120,1152]{2,1,0:T(8,128)(2,1)} %param.19) | copy-start | bytes 829444
  274.7 5.6 %copy-start.11 = (bf16[8,4,72,120]{3,2,1,0:T(8,128)(2,1)S(1)}, bf16[8,4,72,120]{3,2,1,0:T(8,128)(2,1)}, u32[]{:S(2)}) copy-start(bf16[8,4,72,120]{3,2,1,0:T(8,128)(2,1)} %get-tuple-element.33) | copy-start | bytes 1658884
  280.3 6.6 %copy-start.22 = (pred[120]{0:T(512)(128)(4,1)S(1)}, pred[120]{0:T(512)(128)(4,1)}, u32[]{:S(2)}) copy-start(pred[120]{0:T(512)(128)(4,1)} %copy-done.21) | copy-start | bytes 364
  291.8 1.7 copy-start.2
  291.8 2.5 copy-start.6
  296.2 20.5 %copy-start.20 = (bf16[32]{0:T(256)(128)(2,1)S(1)}, bf16[32]{0:T(256)(128)(2,1)}, u32[]{:S(2)}) copy-start(bf16[32]{0:T(256)(128)(2,1)} %param.35) | copy-start | bytes 196
  296.2 20.5 %copy-start.12 = (bf16[1152,32]{0,1:T(8,128)(2,1)S(1)}, bf16[1152,32]{0,1:T(8,128)(2,1)}, u32[]{:S(2)}) copy-start(bf16[1152,32]{0,1:T(8,128)(2,1)} %param.34) | copy-start | bytes 221188
  296.2 22.5 %copy-start.19 = (f32[2,2]{1,0:T(2,128)S(1)}, f32[2,2]{1,0:T(2,128)}, u32[]{:S(2)}) copy-start(f32[2,2]{1,0:T(2,128)} %param.24) | copy-start | bytes 52
